TPU v7x, 32 devices: a whole 2x2x4 slice. The times are simulated.
32 devices in a mesh: rows: 4 (over z), cols: 8 (over y, x, core).
Axes of the slice: x: 2, y: 2, z: 4, core: 2. Of those that a mesh axis runs over, the one named last changes fastest.
Arguments:
- features: bfloat16 [65536, 440], P(('rows', 'cols')), may hold values from -12 to 12
- residual: float32 [65536, 147], P(('rows', 'cols')), may hold values from -6 to 6
- coeffs: float32 [65536, 147], P(('rows', 'cols')), may hold values from -3 to 3
- block_inverse: float32 [2, 2048, 2048], P(None, ('rows', 'cols')), may hold values from -0.0234375 to 0.0234375
- block_index: int32 [2, 2048], P(None, 'cols'), may hold values from 0 to 2047, as said below
- owners: int32 [2], replicated, may hold values from 0 to 3
Outputs:
- new_coeffs: float32 [65536, 147], P(('rows', 'cols'))
- new_residual: float32 [65536, 147], P(('rows', 'cols'))
Inputs may be any that keep to these rules, and one draw needn't show every extreme that they name: `block_index`: for each step and each aligned run of 256 positions, the indices are distinct.
All inputs are finite; a program needn't handle non-finite values.
Results may differ from a plain program's by a relative error of at most 0.0028.
Values may be sent and summed in bfloat16 or wider, within the bound.
No kernel may reach another device: no remote copies, remote signals or barrier semaphores. Data moves between devices by JAX's collectives and lax.ppermute only.
A program may use at most 64 MiB of HBM per device.

v0:
```python
import jax
import jax.numpy as jnp
from jax import lax
from jax.sharding import PartitionSpec as P

penalty = 0.5


def from_root(value, axis, source):
    kept = jnp.where(lax.axis_index(axis) == source, value, 0).astype(value.dtype)
    return lax.psum(kept, axis)


def per_device(features, residual, coeffs, block_inverse, block_index, owners):
    frame_count = features.shape[0]
    feature_width = features.shape[1]
    per_col = block_index.shape[1]
    row_block = min(512, frame_count)
    exponent = -1.0 / feature_width
    my_row = lax.axis_index("rows")
    my_col = lax.axis_index("cols")
    squares = jnp.sum(jnp.square(features.astype(jnp.float32)), axis=1)
    feature_blocks = features.reshape(frame_count // row_block, row_block, feature_width)
    norm_blocks = squares.reshape(frame_count // row_block, row_block)
    for step_id in range(block_index.shape[0]):
        chosen_rows = block_index[step_id]
        owner_row = owners[step_id]
        mine_feat = jnp.take(features, chosen_rows, axis=0)
        mine_res = jnp.take(residual, chosen_rows, axis=0)
        row_piece = from_root(mine_feat, "rows", owner_row)
        chosen = lax.all_gather(row_piece, "cols", axis=0, tiled=True)
        res_piece = from_root(mine_res, "rows", owner_row)
        picked_res = lax.all_gather(res_piece, "cols", axis=0, tiled=True)
        my_update = jnp.dot(
            block_inverse[step_id],
            picked_res,
            precision=lax.Precision.HIGHEST,
            preferred_element_type=jnp.float32,
        ).astype(jnp.bfloat16)
        update = lax.all_gather(my_update, ("rows", "cols"), axis=0, tiled=True)
        chosen_norms = jnp.sum(jnp.square(chosen.astype(jnp.float32)), axis=1)

        def kernel_rows(operands):
            block_rows, block_norms = operands
            inner = lax.dot_general(
                block_rows, chosen, (((1,), (1,)), ((), ())), preferred_element_type=jnp.float32
            )
            distance = block_norms[:, None] + chosen_norms[None, :] - 2.0 * inner
            kernel = jnp.exp(distance * exponent).astype(jnp.bfloat16)
            return jnp.dot(kernel, update, preferred_element_type=jnp.float32)

        change = lax.map(kernel_rows, (feature_blocks, norm_blocks)).reshape(frame_count, -1)
        residual = residual - change
        is_owner = jnp.where(my_row == owner_row, 1.0, 0.0).astype(jnp.float32)
        mine_update = (
            lax.dynamic_slice_in_dim(update, my_col * per_col, per_col, 0).astype(jnp.float32)
            * is_owner
        )
        residual = residual.at[chosen_rows].add(-penalty * mine_update)
        coeffs = coeffs.at[chosen_rows].add(mine_update)
    return (coeffs, residual)


def solution(mesh):
    in_specs = (
        P(("rows", "cols"), None),
        P(("rows", "cols"), None),
        P(("rows", "cols"), None),
        P(None, ("rows", "cols"), None),
        P(None, "cols"),
        P(),
    )
    out_specs = (P(("rows", "cols"), None), P(("rows", "cols"), None))
    return jax.shard_map(
        per_device, mesh=mesh, in_specs=in_specs, out_specs=out_specs, check_vma=False
    )
```

profile of v0, /device:TPU:0, one launch (start us, length us, event | category | flops | bytes accessed | tf_op | source)
XLA Modules:
  0.0 380.8 jit_solution(9416683391688885127)
XLA Ops:
  13.6 3.8 %copy.18 = bf16[2048,440]{1,0:T(8,128)(2,1)} copy(bf16[2048,440]{0,1:T(8,128)(2,1)} %param.14) | data formatting | bytes 3604480 | tf_op args[0]
  20.6 3.2 gather_fusion.3
  25.6 26.5 %all-reduce.5.cloned.1.call-done = f32[256,147]{1,0:T(8,128)} async-done(((f32[256,147]{1,0:T(8,128)}), f32[256,147]{1,0:T(8,128)}) %all-reduce.5.cloned.1.call-update) | async-done | bytes 150544 | tf_op jit(solution)/shard_map/psum | solution.py:11
  52.1 41.4 %all-reduce.9.cloned.1.call-done = (bf16[256,440]{1,0:T(8,128)(2,1)}, bf16[256,440]{1,0:T(8,128)(2,1)}) async-done(((bf16[256,440]{1,0:T(8,128)(2,1)}, bf16[256,440]{1,0:T(8,128)(2,1)}), (bf16[256,440]{1,0:T(8,128)(2,1)}, bf16[256,440]{1,0:T(8,128)(2,1)})) %all-reduce.9.cloned.1.call-update) | async-done | bytes 450576 | tf_op jit(solution)/shard_map/psum | solution.py:11
  94.0 29.0 %all-gather.5.cloned.1.call-done = f32[2048,147]{1,0:T(8,128)} async-done(((f32[256,147]{1,0:T(8,128)}), f32[2048,147]{1,0:T(8,128)}) %all-gather.5.cloned.1.call-update) | async-done | bytes 1204240 | tf_op jit(solution)/shard_map/all_gather | solution.py:33
  126.0 46.2 %all_gather.19 = bf16[2048,147]{1,0:T(8,128)(2,1)} all-gather(bf16[64,147]{1,0:T(8,128)(2,1)S(1)} %fusion.18), channel_id=1, replica_groups=mesh['rows'=4,'cols'=8] {'rows','cols'}, dimensions={0}, use_global_device_ids=true | all-gather | bytes 620928 | tf_op jit(solution)/shard_map/all_gather | solution.py:40
  174.6 14.1 %while.20 = (s32[]{:T(128)}, f32[4,512,147]{1,2,0:T(8,128)S(1)}, f32[4,512]{1,0:T(4,128)S(1)}, f32[2048]{0:T(1024)S(1)}, bf16[4,512,440]{2,1,0:T(8,128)(2,1)}, /...) while((s32[]{:T(128)}, f32[4,512,147]{1,2,0:T(8,128)S(1)}, f32[4,512]{1,0:T(4,128)S(1)}, ...), condition=%wide.region_6.9_spmd, body=%wide.region_5.8_spmd.sunk | while | flops 1236271104 | bytes 3996761 | solution.py:52
  174.6 3.5 fusion.59
  178.2 3.5 fusion.59
  181.7 3.5 fusion.59
  185.2 3.5 fusion.59
  193.0 3.1 scatter_custom_fusion.1
  200.4 31.0 %all-reduce.7.cloned.1.call-done = f32[256,147]{1,0:T(8,128)} async-done(((f32[256,147]{1,0:T(8,128)}), f32[256,147]{1,0:T(8,128)}) %all-reduce.7.cloned.1.call-update) | async-done | bytes 150544 | tf_op jit(solution)/shard_map/psum | solution.py:11
  233.3 5.2 %scatter_custom_fusion = f32[2048,147]{1,0:T(8,128)} fusion(f32[2048,147]{1,0:T(8,128)} %copy.17, s32[256]{0:T(256)S(1)} %bitcast.79, f32[]{:T(128)S(6)} %select_n.78, bf16[2048,147]{1,0:T(8,128)(2,1)} %get-tuple-element.271, s32[]{:T(128)S(6)} %select_n.77, s32[]{:T(128)} %constant.43.clone.1), kind=kCustom, calls=%fused_computation.50 | custom fusion | flops 112896 | bytes 1335816 | tf_op jit(solution)/shard_map/scatter-add | solution.py:60
  238.5 22.4 %all-gather.11.cloned.1.call-done = bf16[2048,440]{1,0:T(8,128)(2,1)} async-done(((bf16[256,440]{1,0:T(8,128)(2,1)}), bf16[2048,440]{1,0:T(8,128)(2,1)}) %all-gather.11.cloned.1.call-update) | async-done | bytes 1802256 | tf_op jit(solution)/shard_map/all_gather | solution.py:31
  263.0 27.6 %all-gather.9.cloned.1.call-done = f32[2048,147]{1,0:T(8,128)} async-done(((f32[256,147]{1,0:T(8,128)}), f32[2048,147]{1,0:T(8,128)}) %all-gather.9.cloned.1.call-update) | async-done | bytes 1204240 | tf_op jit(solution)/shard_map/all_gather | solution.py:33
  293.5 46.1 %all_gather.22 = bf16[2048,147]{1,0:T(8,128)(2,1)} all-gather(bf16[64,147]{1,0:T(8,128)(2,1)S(1)} %fusion.19), channel_id=1, replica_groups=mesh['rows'=4,'cols'=8] {'rows','cols'}, dimensions={0}, use_global_device_ids=true | all-gather | bytes 620928 | tf_op jit(solution)/shard_map/all_gather | solution.py:40
  339.7 16.6 %while.21 = (s32[]{:T(128)}, f32[4,512,147]{1,2,0:T(8,128)S(1)}, f32[4,512]{1,0:T(4,128)S(1)}, f32[2048]{0:T(1024)S(1)}, bf16[4,512,440]{2,1,0:T(8,128)(2,1)}, /...) while((s32[]{:T(128)}, f32[4,512,147]{1,2,0:T(8,128)S(1)}, f32[4,512]{1,0:T(4,128)S(1)}, ...), condition=%wide.region_13.16_spmd, body=%wide.region_12.15_spmd.sunk | while | flops 1236271104 | bytes 3996761 | solution.py:52
  339.7 4.1 %fusion.63 = f32[4,512,147]{1,2,0:T(8,128)S(1)} fusion(f32[4,512,147]{1,2,0:T(8,128)S(1)} %get-tuple-element.241, s32[]{:T(128)} %get-tuple-element.240, bf16[2048,147]{1,0:T(8,128)(2,1)} %get-tuple-element.254, bf16[2048,440]{1,0:T(8,128)(2,1)} %get-tuple-element.253, f32[2048]{0:T(1024)S(1)} %get-tuple-element.251, f32[512]{0:T(512)S(1)} %bitcast.71, ...), kind=kOutput, calls=%fused_computation.19.clone.1 | convolution fusion | flops 1236271104 | bytes 3992576 | tf_op jit(solution)/shard_map/while/body/eval_jaxpr/dot_general | solution.py:50
  343.9 4.1 %fusion.63 = f32[4,512,147]{1,2,0:T(8,128)S(1)} fusion(f32[4,512,147]{1,2,0:T(8,128)S(1)} %get-tuple-element.241, s32[]{:T(128)} %get-tuple-element.240, bf16[2048,147]{1,0:T(8,128)(2,1)} %get-tuple-element.254, bf16[2048,440]{1,0:T(8,128)(2,1)} %get-tuple-element.253, f32[2048]{0:T(1024)S(1)} %get-tuple-element.251, f32[512]{0:T(512)S(1)} %bitcast.71, ...), kind=kOutput, calls=%fused_computation.19.clone.1 | convolution fusion | flops 1236271104 | bytes 3992576 | tf_op jit(solution)/shard_map/while/body/eval_jaxpr/dot_general | solution.py:50
  348.1 4.1 %fusion.63 = f32[4,512,147]{1,2,0:T(8,128)S(1)} fusion(f32[4,512,147]{1,2,0:T(8,128)S(1)} %get-tuple-element.241, s32[]{:T(128)} %get-tuple-element.240, bf16[2048,147]{1,0:T(8,128)(2,1)} %get-tuple-element.254, bf16[2048,440]{1,0:T(8,128)(2,1)} %get-tuple-element.253, f32[2048]{0:T(1024)S(1)} %get-tuple-element.251, f32[512]{0:T(512)S(1)} %bitcast.71, ...), kind=kOutput, calls=%fused_computation.19.clone.1 | convolution fusion | flops 1236271104 | bytes 3992576 | tf_op jit(solution)/shard_map/while/body/eval_jaxpr/dot_general | solution.py:50
  352.2 4.1 %fusion.63 = f32[4,512,147]{1,2,0:T(8,128)S(1)} fusion(f32[4,512,147]{1,2,0:T(8,128)S(1)} %get-tuple-element.241, s32[]{:T(128)} %get-tuple-element.240, bf16[2048,147]{1,0:T(8,128)(2,1)} %get-tuple-element.254, bf16[2048,440]{1,0:T(8,128)(2,1)} %get-tuple-element.253, f32[2048]{0:T(1024)S(1)} %get-tuple-element.251, f32[512]{0:T(512)S(1)} %bitcast.71, ...), kind=kOutput, calls=%fused_computation.19.clone.1 | convolution fusion | flops 1236271104 | bytes 3992576 | tf_op jit(solution)/shard_map/while/body/eval_jaxpr/dot_general | solution.py:50
  358.1 3.2 bitcast_subtract_fusion
  361.3 5.1 %scatter_custom_fusion.3 = f32[2048,147]{1,0:T(8,128)} fusion(f32[2048,147]{1,0:T(8,128)} %bitcast_subtract_fusion, s32[256]{0:T(256)S(1)} %bitcast.76, f32[]{:T(128)S(6)} %select_n.84, f32[]{:T(128)} %constant.72.clone.1, bf16[2048,147]{1,0:T(8,128)(2,1)} %get-tuple-element.272, s32[]{:T(128)S(6)} %select_n.77, s32[]{:T(128)} %constant.43.clone.1), kind=kCustom, calls=%fused_computation.43 | custom fusion | flops 150528 | bytes 1336328 | tf_op jit(solution)/shard_map/scatter-add | solution.py:59
  (70 shorter events, 40.6 us)
Async XLA Ops:
  7.2 44.9 %all-reduce.5.cloned.1.call-start = ((), (), s32[]{:S(2)}) async-start(), calls=%async_computation | async-start | bytes 524288 | tf_op jit(solution)/shard_map/psum | solution.py:11
  11.1 6.4 %copy-start = (f32[2048,147]{1,0:T(8,128)}, f32[2048,147]{1,0:T(8,128)S(1)}, u32[]{:S(2)}) copy-start(f32[2048,147]{1,0:T(8,128)S(1)} %copy.16) | copy-start | bytes 3612676
  13.6 80.0 %all-reduce.9.cloned.1.call-start = ((), (), s32[]{:S(2)}) async-start(), calls=%async_computation.6 | async-start | bytes 1048576 | tf_op jit(solution)/shard_map/psum | solution.py:11
  20.5 73.1 %copy-start.2 = (bf16[2048,440]{0,1:T(8,128)(2,1)S(1)}, bf16[2048,440]{0,1:T(8,128)(2,1)}, u32[]{:S(2)}) copy-start(bf16[2048,440]{0,1:T(8,128)(2,1)} %param.14) | copy-start | bytes 5406724
  23.8 70.2 %copy-start.7 = (s32[2,256]{1,0:T(2,128)S(1)}, s32[2,256]{1,0:T(2,128)}, u32[]{:S(2)}) copy-start(s32[2,256]{1,0:T(2,128)} %param.18) | copy-start | bytes 6148
  23.8 99.3 %copy-start.5 = (f32[2,64,2048]{2,1,0:T(8,128)S(1)}, f32[2,64,2048]{2,1,0:T(8,128)}, u32[]{:S(2)}) copy-start(f32[2,64,2048]{2,1,0:T(8,128)} %param.17) | copy-start | bytes 3145732
  25.5 97.5 %all-gather.5.cloned.1.call-start = ((), (), s32[]{:S(2)}) async-start(), calls=%async_computation.1 | async-start | bytes 2359296 | tf_op jit(solution)/shard_map/all_gather | solution.py:33
  52.1 120.1 %all-gather.7.cloned.1.call-start = ((), (), s32[]{:S(2)}) async-start(), calls=%async_computation.2 | async-start | bytes 2359296 | tf_op jit(solution)/shard_map/all_gather | solution.py:31
  93.6 137.9 %all-reduce.7.cloned.1.call-start = ((), (), s32[]{:S(2)}) async-start(), calls=%async_computation.3 | async-start | bytes 524288 | tf_op jit(solution)/shard_map/psum | solution.py:11
  172.2 2.4 copy-start.3
  196.1 35.3 %copy-start.4 = (f32[2048,147]{0,1:T(8,128)S(1)}, f32[2048,147]{0,1:T(8,128)}, u32[]{:S(2)}) copy-start(f32[2048,147]{0,1:T(8,128)} %param.16) | copy-start | bytes 3612676
  199.6 61.3 %all-gather.11.cloned.1.call-start = ((), (), s32[]{:S(2)}) async-start(), calls=%async_computation.5 | async-start | bytes 2359296 | tf_op jit(solution)/shard_map/all_gather | solution.py:31
  200.2 90.4 %all-gather.9.cloned.1.call-start = ((), (), s32[]{:S(2)}) async-start(), calls=%async_computation.4 | async-start | bytes 2359296 | tf_op jit(solution)/shard_map/all_gather | solution.py:33
  233.3 57.3 %copy-start.6 = (f32[2,64,2048]{2,1,0:T(8,128)S(1)}, f32[2,64,2048]{2,1,0:T(8,128)}, u32[]{:S(2)}) copy-start(f32[2,64,2048]{2,1,0:T(8,128)} %param.17) | copy-start | bytes 3145732
  366.4 2.8 copy-start.1
Sparse Core Ops, SparseCore 0:
  13.7 38.3 all-reduce.4
  55.0 38.4 all-reduce.8
  95.4 27.5 all-gather.4
  124.8 31.5 all-gather.6
  199.7 31.6 all-reduce.6
  233.2 27.6 all-gather.10
  262.8 27.7 all-gather.8
where the time goes:
time: 382 us; the launch traced here: 381 us
  waiting for transfers between devices  179 us (47%)
  blocking collectives  92.3 us (24%)
  matrix products  36.3 us (10%)
  other arithmetic  30.5 us (8%)
  local copies, waits for them, and re-layouts  26.8 us (7%)
  between operations  15.7 us (4%)
    psum x3, waiting for transfers between devices, from_root(): return lax.psum(kept, axis)  98.9 us
    all_gather x2, blocking collectives, per_device(): update = lax.all_gather(my_update, ('rows', 'cols'), axis=0, tiled=True)  92.3 us
    all_gather x2, waiting for transfers between devices, per_device(): picked_res = lax.all_gather(res_piece, 'cols', axis=0, tiled=True)  56.6 us
    dot_general x8, matrix products, kernel_rows(): return jnp.dot(kernel, update, preferred_element_type=jnp.float32)  30.5 us
    all_gather x2, waiting for transfers between devices, per_device(): chosen = lax.all_gather(row_piece, 'cols', axis=0, tiled=True)  22.4 us
    unnamed x21, local copies, waits for them, and re-layouts  11.9 us
    scatter-add x2, other arithmetic, per_device(): coeffs = coeffs.at[chosen_rows].add(mine_update)  8.29 us
    scatter-add x2, other arithmetic, per_device(): residual = residual.at[chosen_rows].add(-penalty * mine_update)  8.22 us
  transfers between devices with their start and end apart: 7, of which 6 were waited for; matrix products, arithmetic and copies ran while one was open for 6% of the time, Pallas kernels for 0%

commit v1 on v0

--- a/solution.py
+++ b/solution.py
@@ -37,7 +37,18 @@
             precision=lax.Precision.HIGHEST,
             preferred_element_type=jnp.float32,
         ).astype(jnp.bfloat16)
-        update = lax.all_gather(my_update, ("rows", "cols"), axis=0, tiled=True)
+        opened = lax.axis_size(("rows", "cols"))
+        m_next = lax.axis_index(("rows", "cols"))
+        e_now, response = (opened, m_next)
+        update, w_next = (my_update, 1)
+        while w_next < e_now:
+            val2 = lax.ppermute(
+                update, ("rows", "cols"), [(kk, kk ^ w_next) for kk in range(e_now)]
+            )
+            arr_now = jnp.concatenate([update, val2], axis=0)
+            reached = jnp.concatenate([val2, update], axis=0)
+            update = jnp.where(response & w_next == 0, arr_now, reached)
+            w_next = 2 * w_next
         chosen_norms = jnp.sum(jnp.square(chosen.astype(jnp.float32)), axis=1)
 
         def kernel_rows(operands):

time: 382 us -> 347 us (0.908)
  blocking collectives: 92.3 us -> 0 us
  waiting for transfers between devices: 179 us -> 217 us
  starting transfers between devices: 0.46 us -> 17.7 us
    all_gather x2 -> x0, blocking collectives: 92.3 us -> none  [per_device(): update = lax.all_gather(my_update, ('rows', 'cols'), axis=0, tiled=True)]
    ppermute x0 -> x10, waiting for transfers between devices: none -> 54.1 us  [per_device(): lax.ppermute(update, ('rows', 'cols'), [(kk, kk ^ w_next) for kk in range...]
    all_gather x2, waiting for transfers between devices: 22.4 us -> 0.01 us  [per_device(): chosen = lax.all_gather(row_piece, 'cols', axis=0, tiled=True)]
    ppermute x0 -> x10, starting transfers between devices: none -> 17.2 us  [per_device(): lax.ppermute(update, ('rows', 'cols'), [(kk, kk ^ w_next) for kk in range...]
    psum x3, waiting for transfers between devices: 98.9 us -> 104 us  [from_root(): return lax.psum(kept, axis)]
    unnamed x21 -> x19, local copies, waits for them, and re-layouts: 11.9 us -> 12.9 us
  transfers between devices with their start and end apart: 7 -> 17, of which waited for: 6 -> 15; matrix products, arithmetic and copies ran while one was open for 6% -> 8% of each run, Pallas kernels for 0% -> 0%
where the time goes in v1:
time: 347 us
  waiting for transfers between devices  217 us (63%)
  matrix products  36.3 us (10%)
  other arithmetic  32.6 us (9%)
  local copies, waits for them, and re-layouts  27.1 us (8%)
  starting transfers between devices  17.7 us (5%)
  between operations  15.7 us (5%)
    psum x3, waiting for transfers between devices, from_root(): return lax.psum(kept, axis)  104 us
    all_gather x2, waiting for transfers between devices, per_device(): picked_res = lax.all_gather(res_piece, 'cols', axis=0, tiled=True)  58.1 us
    ppermute x10, waiting for transfers between devices, per_device(): lax.ppermute(update, ('rows', 'cols'), [(kk, kk ^ w_next) for kk in range...  54.1 us
    dot_general x8, matrix products, kernel_rows(): return jnp.dot(kernel, update, preferred_element_type=jnp.float32)  30.4 us
    ppermute x10, starting transfers between devices, per_device(): lax.ppermute(update, ('rows', 'cols'), [(kk, kk ^ w_next) for kk in range...  17.2 us
    unnamed x19, local copies, waits for them, and re-layouts  12.9 us
    scatter-add x2, other arithmetic, per_device(): residual = residual.at[chosen_rows].add(-penalty * mine_update)  8.2 us
    scatter-add x2, other arithmetic, per_device(): coeffs = coeffs.at[chosen_rows].add(mine_update)  8.2 us
  transfers between devices with their start and end apart: 17, of which 15 were waited for; matrix products, arithmetic and copies ran while one was open for 8% of the time, Pallas kernels for 0%

profile of v1, /device:TPU:0, one launch (start us, length us, event | category | flops | bytes accessed | tf_op | source)
XLA Modules:
  0.0 346.6 jit_solution(13817953129405108673)
XLA Ops:
  14.3 3.8 %copy.18 = bf16[2048,440]{1,0:T(8,128)(2,1)} copy(bf16[2048,440]{0,1:T(8,128)(2,1)} %param.14) | data formatting | bytes 3604480 | tf_op args[0]
  25.4 26.6 %all-reduce.5.cloned.1.call-done = f32[256,147]{1,0:T(8,128)} async-done(((f32[256,147]{1,0:T(8,128)}), f32[256,147]{1,0:T(8,128)}) %all-reduce.5.cloned.1.call-update) | async-done | bytes 150544 | tf_op jit(solution)/shard_map/psum | solution.py:11
  52.1 41.4 %all-reduce.9.cloned.1.call-done = (bf16[256,440]{1,0:T(8,128)(2,1)}, bf16[256,440]{1,0:T(8,128)(2,1)}) async-done(((bf16[256,440]{1,0:T(8,128)(2,1)}, bf16[256,440]{1,0:T(8,128)(2,1)}), (bf16[256,440]{1,0:T(8,128)(2,1)}, bf16[256,440]{1,0:T(8,128)(2,1)})) %all-reduce.9.cloned.1.call-update) | async-done | bytes 450576 | tf_op jit(solution)/shard_map/psum | solution.py:11
  93.6 29.5 %all-gather.5.cloned.1.call-done = f32[2048,147]{1,0:T(8,128)} async-done(((f32[256,147]{1,0:T(8,128)}), f32[2048,147]{1,0:T(8,128)}) %all-gather.5.cloned.1.call-update) | async-done | bytes 1204240 | tf_op jit(solution)/shard_map/all_gather | solution.py:33
  133.1 6.1 %collective-permute-done.2 = bf16[256,147]{1,0:T(8,128)(2,1)S(1)} collective-permute-done((bf16[256,147]{1,0:T(8,128)(2,1)S(1)}, bf16[256,147]{1,0:T(8,128)(2,1)S(1)}, u32[]{:S(2)}, u32[]{:S(2)}) %collective-permute-start.2) | collective-permute-done | bytes 75296 | tf_op jit(solution)/shard_map/ppermute | solution.py:45
  140.8 5.9 %collective-permute-done.3 = bf16[512,147]{1,0:T(8,128)(2,1)S(1)} collective-permute-done((bf16[512,147]{1,0:T(8,128)(2,1)S(1)}, bf16[512,147]{1,0:T(8,128)(2,1)S(1)}, u32[]{:S(2)}, u32[]{:S(2)}) %collective-permute-start.3) | collective-permute-done | bytes 150560 | tf_op jit(solution)/shard_map/ppermute | solution.py:45
  147.0 3.8 %collective-permute-start.4 = (bf16[1024,147]{1,0:T(8,128)(2,1)S(1)}, bf16[1024,147]{1,0:T(8,128)(2,1)S(1)}, u32[]{:S(2)}, u32[]{:S(2)}) collective-permute-start(bf16[1024,147]{1,0:T(8,128)(2,1)S(1)} %maximum_select_fusion.2), channel_id=1, source_target_pairs={{0,16},{1,17},{2,18},{3,19},{4,20},{5,21},{6,22},{7,23},{8,24},{9,... | collective-permute-start | bytes 903176 | tf_op jit(solution)/shard_map/ppermute | solution.py:45
  151.2 16.3 %collective-permute-done.4 = bf16[1024,147]{1,0:T(8,128)(2,1)S(1)} collective-permute-done((bf16[1024,147]{1,0:T(8,128)(2,1)S(1)}, bf16[1024,147]{1,0:T(8,128)(2,1)S(1)}, u32[]{:S(2)}, u32[]{:S(2)}) %collective-permute-start.4) | collective-permute-done | bytes 301088 | tf_op jit(solution)/shard_map/ppermute | solution.py:45
  171.1 14.1 %while.20 = (s32[]{:T(128)}, f32[4,512,147]{1,2,0:T(8,128)S(1)}, f32[4,512]{1,0:T(4,128)S(1)}, f32[2048]{0:T(1024)S(1)}, bf16[4,512,440]{2,1,0:T(8,128)(2,1)}, /...) while((s32[]{:T(128)}, f32[4,512,147]{1,2,0:T(8,128)S(1)}, f32[4,512]{1,0:T(4,128)S(1)}, ...), condition=%wide.region_6.9_spmd, body=%wide.region_5.8_spmd.sunk | while | flops 1236271104 | bytes 3996761 | solution.py:63
  171.2 3.5 %fusion.59 = f32[4,512,147]{1,2,0:T(8,128)S(1)} fusion(f32[4,512,147]{1,2,0:T(8,128)S(1)} %get-tuple-element.217, s32[]{:T(128)} %get-tuple-element.216, bf16[2048,147]{1,0:T(8,128)(2,1)} %get-tuple-element.230, bf16[2048,440]{1,0:T(8,128)(2,1)S(1)} %get-tuple-element.229, f32[2048]{0:T(1024)S(1)} %get-tuple-element.227, f32[512]{0:T(512)S(1)} %bitcast.70, ...), kind=kOutput, calls=%fused_computation.10.clone.1 | convolution fusion | flops 1236271104 | bytes 3992576 | tf_op jit(solution)/shard_map/while/body/eval_jaxpr/dot_general | solution.py:61
  174.7 3.5 %fusion.59 = f32[4,512,147]{1,2,0:T(8,128)S(1)} fusion(f32[4,512,147]{1,2,0:T(8,128)S(1)} %get-tuple-element.217, s32[]{:T(128)} %get-tuple-element.216, bf16[2048,147]{1,0:T(8,128)(2,1)} %get-tuple-element.230, bf16[2048,440]{1,0:T(8,128)(2,1)S(1)} %get-tuple-element.229, f32[2048]{0:T(1024)S(1)} %get-tuple-element.227, f32[512]{0:T(512)S(1)} %bitcast.70, ...), kind=kOutput, calls=%fused_computation.10.clone.1 | convolution fusion | flops 1236271104 | bytes 3992576 | tf_op jit(solution)/shard_map/while/body/eval_jaxpr/dot_general | solution.py:61
  194.5 36.2 %all-reduce.7.cloned.1.call-done = f32[256,147]{1,0:T(8,128)} async-done(((f32[256,147]{1,0:T(8,128)}), f32[256,147]{1,0:T(8,128)}) %all-reduce.7.cloned.1.call-update) | async-done | bytes 150544 | tf_op jit(solution)/shard_map/psum | solution.py:11
  231.5 28.6 %all-gather.9.cloned.1.call-done = f32[2048,147]{1,0:T(8,128)} async-done(((f32[256,147]{1,0:T(8,128)}), f32[2048,147]{1,0:T(8,128)}) %all-gather.9.cloned.1.call-update) | async-done | bytes 1204240 | tf_op jit(solution)/shard_map/all_gather | solution.py:33
  270.2 6.2 %collective-permute-done.7 = bf16[256,147]{1,0:T(8,128)(2,1)S(1)} collective-permute-done((bf16[256,147]{1,0:T(8,128)(2,1)S(1)}, bf16[256,147]{1,0:T(8,128)(2,1)S(1)}, u32[]{:S(2)}, u32[]{:S(2)}) %collective-permute-start.7) | collective-permute-done | bytes 75296 | tf_op jit(solution)/shard_map/ppermute | solution.py:45
  278.0 6.4 %collective-permute-done.8 = bf16[512,147]{1,0:T(8,128)(2,1)S(1)} collective-permute-done((bf16[512,147]{1,0:T(8,128)(2,1)S(1)}, bf16[512,147]{1,0:T(8,128)(2,1)S(1)}, u32[]{:S(2)}, u32[]{:S(2)}) %collective-permute-start.8) | collective-permute-done | bytes 150560 | tf_op jit(solution)/shard_map/ppermute | solution.py:45
  284.6 3.8 %collective-permute-start.9 = (bf16[1024,147]{1,0:T(8,128)(2,1)S(1)}, bf16[1024,147]{1,0:T(8,128)(2,1)S(1)}, u32[]{:S(2)}, u32[]{:S(2)}) collective-permute-start(bf16[1024,147]{1,0:T(8,128)(2,1)S(1)} %maximum_select_fusion.3), channel_id=1, source_target_pairs={{0,16},{1,17},{2,18},{3,19},{4,20},{5,21},{6,22},{7,23},{8,24},{9,... | collective-permute-start | bytes 903176 | tf_op jit(solution)/shard_map/ppermute | solution.py:45
  291.1 5.1 %scatter_custom_fusion = f32[2048,147]{1,0:T(8,128)} fusion(f32[2048,147]{1,0:T(8,128)} %copy.17, s32[256]{0:T(256)S(1)} %bitcast.79, f32[]{:T(128)S(6)} %select_n.148, bf16[2048,147]{1,0:T(8,128)(2,1)} %get-tuple-element.273, s32[]{:T(128)S(6)} %select_n.147, s32[]{:T(128)} %constant.31.clone.1), kind=kCustom, calls=%fused_computation.56 | custom fusion | flops 112896 | bytes 1335816 | tf_op jit(solution)/shard_map/scatter-add | solution.py:71
  298.3 5.8 %collective-permute-done.9 = bf16[1024,147]{1,0:T(8,128)(2,1)S(1)} collective-permute-done((bf16[1024,147]{1,0:T(8,128)(2,1)S(1)}, bf16[1024,147]{1,0:T(8,128)(2,1)S(1)}, u32[]{:S(2)}, u32[]{:S(2)}) %collective-permute-start.9) | collective-permute-done | bytes 301088 | tf_op jit(solution)/shard_map/ppermute | solution.py:45
  305.5 16.6 %while.21 = (s32[]{:T(128)}, f32[4,512,147]{1,2,0:T(8,128)S(1)}, f32[4,512]{1,0:T(4,128)S(1)}, f32[2048]{0:T(1024)S(1)}, bf16[4,512,440]{2,1,0:T(8,128)(2,1)}, /...) while((s32[]{:T(128)}, f32[4,512,147]{1,2,0:T(8,128)S(1)}, f32[4,512]{1,0:T(4,128)S(1)}, ...), condition=%wide.region_13.16_spmd, body=%wide.region_12.15_spmd.sunk | while | flops 1236271104 | bytes 3996761 | solution.py:63
  305.5 4.1 %fusion.63 = f32[4,512,147]{1,2,0:T(8,128)S(1)} fusion(f32[4,512,147]{1,2,0:T(8,128)S(1)} %get-tuple-element.241, s32[]{:T(128)} %get-tuple-element.240, bf16[2048,147]{1,0:T(8,128)(2,1)} %get-tuple-element.254, bf16[2048,440]{1,0:T(8,128)(2,1)} %get-tuple-element.253, f32[2048]{0:T(1024)S(1)} %get-tuple-element.251, f32[512]{0:T(512)S(1)} %bitcast.71, ...), kind=kOutput, calls=%fused_computation.19.clone.1 | convolution fusion | flops 1236271104 | bytes 3992576 | tf_op jit(solution)/shard_map/while/body/eval_jaxpr/dot_general | solution.py:61
  309.7 4.1 %fusion.63 = f32[4,512,147]{1,2,0:T(8,128)S(1)} fusion(f32[4,512,147]{1,2,0:T(8,128)S(1)} %get-tuple-element.241, s32[]{:T(128)} %get-tuple-element.240, bf16[2048,147]{1,0:T(8,128)(2,1)} %get-tuple-element.254, bf16[2048,440]{1,0:T(8,128)(2,1)} %get-tuple-element.253, f32[2048]{0:T(1024)S(1)} %get-tuple-element.251, f32[512]{0:T(512)S(1)} %bitcast.71, ...), kind=kOutput, calls=%fused_computation.19.clone.1 | convolution fusion | flops 1236271104 | bytes 3992576 | tf_op jit(solution)/shard_map/while/body/eval_jaxpr/dot_general | solution.py:61
  313.8 4.1 %fusion.63 = f32[4,512,147]{1,2,0:T(8,128)S(1)} fusion(f32[4,512,147]{1,2,0:T(8,128)S(1)} %get-tuple-element.241, s32[]{:T(128)} %get-tuple-element.240, bf16[2048,147]{1,0:T(8,128)(2,1)} %get-tuple-element.254, bf16[2048,440]{1,0:T(8,128)(2,1)} %get-tuple-element.253, f32[2048]{0:T(1024)S(1)} %get-tuple-element.251, f32[512]{0:T(512)S(1)} %bitcast.71, ...), kind=kOutput, calls=%fused_computation.19.clone.1 | convolution fusion | flops 1236271104 | bytes 3992576 | tf_op jit(solution)/shard_map/while/body/eval_jaxpr/dot_general | solution.py:61
  318.0 4.1 %fusion.63 = f32[4,512,147]{1,2,0:T(8,128)S(1)} fusion(f32[4,512,147]{1,2,0:T(8,128)S(1)} %get-tuple-element.241, s32[]{:T(128)} %get-tuple-element.240, bf16[2048,147]{1,0:T(8,128)(2,1)} %get-tuple-element.254, bf16[2048,440]{1,0:T(8,128)(2,1)} %get-tuple-element.253, f32[2048]{0:T(1024)S(1)} %get-tuple-element.251, f32[512]{0:T(512)S(1)} %bitcast.71, ...), kind=kOutput, calls=%fused_computation.19.clone.1 | convolution fusion | flops 1236271104 | bytes 3992576 | tf_op jit(solution)/shard_map/while/body/eval_jaxpr/dot_general | solution.py:61
  327.1 5.1 %scatter_custom_fusion.3 = f32[2048,147]{1,0:T(8,128)} fusion(f32[2048,147]{1,0:T(8,128)} %bitcast_subtract_fusion, s32[256]{0:T(256)S(1)} %bitcast.76, f32[]{:T(128)S(6)} %select_n.159, f32[]{:T(128)} %constant.82.clone.1, bf16[2048,147]{1,0:T(8,128)(2,1)} %get-tuple-element.274, s32[]{:T(128)S(6)} %select_n.147, s32[]{:T(128)} %constant.31.clone.1), kind=kCustom, calls=%fused_computation.49 | custom fusion | flops 150528 | bytes 1336328 | tf_op jit(solution)/shard_map/scatter-add | solution.py:70
  (96 shorter events, 76.9 us)
Async XLA Ops:
  7.2 44.9 %all-reduce.5.cloned.1.call-start = ((), (), s32[]{:S(2)}) async-start(), calls=%async_computation | async-start | bytes 524288 | tf_op jit(solution)/shard_map/psum | solution.py:11
  11.1 7.0 %copy-start = (f32[2048,147]{1,0:T(8,128)}, f32[2048,147]{1,0:T(8,128)S(1)}, u32[]{:S(2)}) copy-start(f32[2048,147]{1,0:T(8,128)S(1)} %copy.16) | copy-start | bytes 3612676
  13.6 80.0 %all-reduce.9.cloned.1.call-start = ((), (), s32[]{:S(2)}) async-start(), calls=%async_computation.6 | async-start | bytes 1048576 | tf_op jit(solution)/shard_map/psum | solution.py:11
  21.2 101.9 %copy-start.4 = (f32[2,64,2048]{2,1,0:T(8,128)S(1)}, f32[2,64,2048]{2,1,0:T(8,128)}, u32[]{:S(2)}) copy-start(f32[2,64,2048]{2,1,0:T(8,128)} %param.17) | copy-start | bytes 3145732
  25.4 97.7 %all-gather.5.cloned.1.call-start = ((), (), s32[]{:S(2)}) async-start(), calls=%async_computation.1 | async-start | bytes 2359296 | tf_op jit(solution)/shard_map/all_gather | solution.py:33
  52.1 116.7 %all-gather.7.cloned.1.call-start = ((), (), s32[]{:S(2)}) async-start(), calls=%async_computation.2 | async-start | bytes 2359296 | tf_op jit(solution)/shard_map/all_gather | solution.py:31
  93.6 57.2 %copy-start.2 = (bf16[2048,440]{0,1:T(8,128)(2,1)S(1)}, bf16[2048,440]{0,1:T(8,128)(2,1)}, u32[]{:S(2)}) copy-start(bf16[2048,440]{0,1:T(8,128)(2,1)} %param.14) | copy-start | bytes 5406724
  93.6 137.1 %all-reduce.7.cloned.1.call-start = ((), (), s32[]{:S(2)}) async-start(), calls=%async_computation.3 | async-start | bytes 524288 | tf_op jit(solution)/shard_map/psum | solution.py:11
  126.0 25.2 %copy-start.6 = (s32[2,256]{1,0:T(2,128)S(1)}, s32[2,256]{1,0:T(2,128)}, u32[]{:S(2)}) copy-start(s32[2,256]{1,0:T(2,128)} %param.18) | copy-start | bytes 6148
  126.0 1.3 collective-permute-start
  127.3 4.3 %collective-permute-start.1 = (bf16[128,147]{1,0:T(8,128)(2,1)S(1)}, bf16[128,147]{1,0:T(8,128)(2,1)S(1)}, u32[]{:S(2)}, u32[]{:S(2)}) collective-permute-start(bf16[128,147]{1,0:T(8,128)(2,1)S(1)} %maximum_select_fusion.8), channel_id=1, source_target_pairs={{0,2},{1,3},{2,0},{3,1},{4,6},{5,7},{6,4},{7,5},{8,10},{9,11},{10,... | collective-permute-start | bytes 112904 | tf_op jit(solution)/shard_map/ppermute | solution.py:45
  131.7 7.5 %collective-permute-start.2 = (bf16[256,147]{1,0:T(8,128)(2,1)S(1)}, bf16[256,147]{1,0:T(8,128)(2,1)S(1)}, u32[]{:S(2)}, u32[]{:S(2)}) collective-permute-start(bf16[256,147]{1,0:T(8,128)(2,1)S(1)} %maximum_select_fusion.6), channel_id=1, source_target_pairs={{0,4},{1,5},{2,6},{3,7},{4,0},{5,1},{6,2},{7,3},{8,12},{9,13},{10,... | collective-permute-start | bytes 225800 | tf_op jit(solution)/shard_map/ppermute | solution.py:45
  139.3 7.5 %collective-permute-start.3 = (bf16[512,147]{1,0:T(8,128)(2,1)S(1)}, bf16[512,147]{1,0:T(8,128)(2,1)S(1)}, u32[]{:S(2)}, u32[]{:S(2)}) collective-permute-start(bf16[512,147]{1,0:T(8,128)(2,1)S(1)} %maximum_select_fusion.4), channel_id=1, source_target_pairs={{0,8},{1,9},{2,10},{3,11},{4,12},{5,13},{6,14},{7,15},{8,0},{9,1},... | collective-permute-start | bytes 451592 | tf_op jit(solution)/shard_map/ppermute | solution.py:45
  147.0 20.5 %collective-permute-start.4 = (bf16[1024,147]{1,0:T(8,128)(2,1)S(1)}, bf16[1024,147]{1,0:T(8,128)(2,1)S(1)}, u32[]{:S(2)}, u32[]{:S(2)}) collective-permute-start(bf16[1024,147]{1,0:T(8,128)(2,1)S(1)} %maximum_select_fusion.2), channel_id=1, source_target_pairs={{0,16},{1,17},{2,18},{3,19},{4,20},{5,21},{6,22},{7,23},{8,24},{9,... | collective-permute-start | bytes 903176 | tf_op jit(solution)/shard_map/ppermute | solution.py:45
  168.7 2.4 copy-start.3
  192.7 67.5 %copy-start.5 = (f32[2,64,2048]{2,1,0:T(8,128)S(1)}, f32[2,64,2048]{2,1,0:T(8,128)}, u32[]{:S(2)}) copy-start(f32[2,64,2048]{2,1,0:T(8,128)} %param.17) | copy-start | bytes 3145732
  194.5 65.7 %all-gather.9.cloned.1.call-start = ((), (), s32[]{:S(2)}) async-start(), calls=%async_computation.4 | async-start | bytes 2359296 | tf_op jit(solution)/shard_map/all_gather | solution.py:33
  230.7 65.5 %all-gather.11.cloned.1.call-start = ((), (), s32[]{:S(2)}) async-start(), calls=%async_computation.5 | async-start | bytes 2359296 | tf_op jit(solution)/shard_map/all_gather | solution.py:31
  263.1 1.3 collective-permute-start.5
  264.3 4.3 %collective-permute-start.6 = (bf16[128,147]{1,0:T(8,128)(2,1)S(1)}, bf16[128,147]{1,0:T(8,128)(2,1)S(1)}, u32[]{:S(2)}, u32[]{:S(2)}) collective-permute-start(bf16[128,147]{1,0:T(8,128)(2,1)S(1)} %maximum_select_fusion.9), channel_id=1, source_target_pairs={{0,2},{1,3},{2,0},{3,1},{4,6},{5,7},{6,4},{7,5},{8,10},{9,11},{10,... | collective-permute-start | bytes 112904 | tf_op jit(solution)/shard_map/ppermute | solution.py:45
  268.7 7.6 %collective-permute-start.7 = (bf16[256,147]{1,0:T(8,128)(2,1)S(1)}, bf16[256,147]{1,0:T(8,128)(2,1)S(1)}, u32[]{:S(2)}, u32[]{:S(2)}) collective-permute-start(bf16[256,147]{1,0:T(8,128)(2,1)S(1)} %maximum_select_fusion.7), channel_id=1, source_target_pairs={{0,4},{1,5},{2,6},{3,7},{4,0},{5,1},{6,2},{7,3},{8,12},{9,13},{10,... | collective-permute-start | bytes 225800 | tf_op jit(solution)/shard_map/ppermute | solution.py:45
  276.4 7.9 %collective-permute-start.8 = (bf16[512,147]{1,0:T(8,128)(2,1)S(1)}, bf16[512,147]{1,0:T(8,128)(2,1)S(1)}, u32[]{:S(2)}, u32[]{:S(2)}) collective-permute-start(bf16[512,147]{1,0:T(8,128)(2,1)S(1)} %maximum_select_fusion.5), channel_id=1, source_target_pairs={{0,8},{1,9},{2,10},{3,11},{4,12},{5,13},{6,14},{7,15},{8,0},{9,1},... | collective-permute-start | bytes 451592 | tf_op jit(solution)/shard_map/ppermute | solution.py:45
  284.6 19.5 %collective-permute-start.9 = (bf16[1024,147]{1,0:T(8,128)(2,1)S(1)}, bf16[1024,147]{1,0:T(8,128)(2,1)S(1)}, u32[]{:S(2)}, u32[]{:S(2)}) collective-permute-start(bf16[1024,147]{1,0:T(8,128)(2,1)S(1)} %maximum_select_fusion.3), channel_id=1, source_target_pairs={{0,16},{1,17},{2,18},{3,19},{4,20},{5,21},{6,22},{7,23},{8,24},{9,... | collective-permute-start | bytes 903176 | tf_op jit(solution)/shard_map/ppermute | solution.py:45
  332.2 2.8 copy-start.1
Sparse Core Ops, SparseCore 0:
  13.7 38.3 all-reduce.4
  55.0 38.4 all-reduce.8
  95.4 27.5 all-gather.4
  124.8 29.1 all-gather.6
  194.6 36.0 all-reduce.6
  232.4 27.6 all-gather.8
  262.0 29.1 all-gather.10
